TPU v7x, 32 devices: a whole 2x2x4 slice. The times are simulated.
32 devices in a mesh: dp: 8 (over z, y), tensor: 4 (over x, core).
Axes of the slice: x: 2, y: 2, z: 4, core: 2. Of those that a mesh axis runs over, the one named last changes fastest.
Arguments:
- inputs: bfloat16 [8, 1024, 2048], P('dp', 'tensor'), may hold values from -6 to 6
- cotangent: bfloat16 [8, 1024, 2048], P('dp', 'tensor'), may hold values from -6 to 6
- lengths: int32 [8], P('dp'), may hold values from 256 to 1024, as said below
- norm1_gain: float32 [2048], replicated, may hold values from 0.5 to 1.5
- w_query: bfloat16 [2048, 2048], P('dp', 'tensor'), may hold values from -0.125 to 0.125
- w_key: bfloat16 [2048, 2048], P('dp', 'tensor'), may hold values from -0.125 to 0.125
- w_value: bfloat16 [2048, 4096], P('dp', 'tensor'), may hold values from -0.125 to 0.125
- w_outgate: bfloat16 [2048, 4096], P('dp', 'tensor'), may hold values from -0.125 to 0.125
- w_beta: bfloat16 [2048, 16], P('dp', 'tensor'), may hold values from -0.125 to 0.125
- w_alpha: bfloat16 [2048, 16], P('dp', 'tensor'), may hold values from -0.125 to 0.125
- conv_query: bfloat16 [128, 16, 4], P('dp', 'tensor'), may hold values from -3 to 3
- conv_key: bfloat16 [128, 16, 4], P('dp', 'tensor'), may hold values from -3 to 3
- conv_value: bfloat16 [256, 16, 4], P('dp', 'tensor'), may hold values from -3 to 3
- a_log: float32 [16], replicated, may hold values from -6.5 to -3
- dt_bias: float32 [16], replicated, may hold values from -1.5 to 0.5
- head_gain: float32 [256], replicated, may hold values from 0.5 to 1.5
- w_out: bfloat16 [2048, 4096], P('dp', 'tensor'), may hold values from -0.125 to 0.125
- norm2_gain: float32 [2048], replicated, may hold values from 0.5 to 1.5
- w_gate: bfloat16 [2048, 5632], P('dp', 'tensor'), may hold values from -0.125 to 0.125
- w_up: bfloat16 [2048, 5632], P('dp', 'tensor'), may hold values from -0.125 to 0.125
- w_down: bfloat16 [2048, 5632], P('dp', 'tensor'), may hold values from -0.109375 to 0.109375
Outputs:
- outputs: bfloat16 [8, 1024, 2048], P('dp', 'tensor')
- grad_inputs: float32 [8, 1024, 2048], P('dp', 'tensor')
- grad_norm1: float32 [2048], replicated
- grad_query: float32 [2048, 2048], P('dp', 'tensor')
- grad_key: float32 [2048, 2048], P('dp', 'tensor')
- grad_value: float32 [2048, 4096], P('dp', 'tensor')
- grad_outgate: float32 [2048, 4096], P('dp', 'tensor')
- grad_beta: float32 [2048, 16], P('dp', 'tensor')
- grad_alpha: float32 [2048, 16], P('dp', 'tensor')
- grad_convq: float32 [128, 16, 4], P('dp', 'tensor')
- grad_convk: float32 [128, 16, 4], P('dp', 'tensor')
- grad_convv: float32 [256, 16, 4], P('dp', 'tensor')
- grad_alog: float32 [16], replicated
- grad_dtbias: float32 [16], replicated
- grad_headgain: float32 [256], replicated
- grad_out: float32 [2048, 4096], P('dp', 'tensor')
- grad_norm2: float32 [2048], replicated
- grad_gate: float32 [2048, 5632], P('dp', 'tensor')
- grad_up: float32 [2048, 5632], P('dp', 'tensor')
- grad_down: float32 [2048, 5632], P('dp', 'tensor')
Inputs may be any that keep to these rules, and one draw needn't show every extreme that they name: `lengths`: each sequence's valid tokens start at its slot's first position; in every draw some sequence fills its whole slot of 1024 positions.
All inputs are finite; a program needn't handle non-finite values.
Results may differ from a plain program's by a relative error of at most 0.025.
Values may be sent and summed in bfloat16 or wider, within the bound.
A program may use at most 320 MiB of HBM per device.

v0:
```python
import jax
import jax.numpy as jnp
from jax import lax
from jax.sharding import PartitionSpec as P

BLOCK = 64


def plain_dot(left_mat, right_mat):
    return jnp.dot(left_mat, right_mat, preferred_element_type=jnp.float32)


def dot_rows(left_mat, right_mat):
    return lax.dot_general(
        left_mat, right_mat, (((1,), (1,)), ((), ())), preferred_element_type=jnp.float32
    )


def dot_tokens(left_mat, right_mat):
    return lax.dot_general(
        left_mat, right_mat, (((0,), (0,)), ((), ())), preferred_element_type=jnp.float32
    )


def rms_apply(values, gain_vec):
    return values * lax.rsqrt(jnp.mean(values * values, axis=-1, keepdims=True) + 1e-05) * gain_vec


def unit_rows(values):
    return values * lax.rsqrt(jnp.sum(values * values, axis=-1, keepdims=True) + 1e-06)


def swiglu(gate_pre, up_pre):
    return jax.nn.silu(gate_pre) * up_pre


def short_conv(values, weight):
    tap_count = weight.shape[2]
    row_count = values.shape[0]
    tap_table = jnp.transpose(weight, (1, 0, 2)).reshape(-1, tap_count)
    padded = jnp.pad(values, ((tap_count - 1, 0), (0, 0)))
    summed = padded[0:row_count] * tap_table[:, 0]
    for tap_index in range(1, tap_count):
        summed = summed + padded[tap_index : tap_index + row_count] * tap_table[:, tap_index]
    return jax.nn.silu(summed)


def block_step(carry_state, pieces):
    query_rows, key_rows, value_rows, beta_rows, decay_rows = pieces
    running = jnp.cumsum(decay_rows, axis=0)
    query_h = jnp.transpose(query_rows, (1, 0, 2))
    key_h = jnp.transpose(key_rows, (1, 0, 2))
    value_h = jnp.transpose(value_rows, (1, 0, 2))
    beta_h = jnp.transpose(beta_rows)
    cum_h = jnp.transpose(running)
    size_c = query_rows.shape[0]
    pos_row = lax.broadcasted_iota(jnp.int32, (size_c, size_c), 0)
    pos_col = lax.broadcasted_iota(jnp.int32, (size_c, size_c), 1)
    lower_inc = pos_row >= pos_col
    lower_strict = pos_row > pos_col
    differ = cum_h[:, :, None] - cum_h[:, None, :]
    within = jnp.where(lower_inc, jnp.exp(jnp.where(lower_inc, differ, 0.0)), 0.0)
    key_key = jnp.einsum("htd,hjd->htj", key_h, key_h, preferred_element_type=jnp.float32)
    coupling = jnp.where(lower_strict, beta_h[:, :, None] * within * key_key, 0.0)
    start_decay = jnp.exp(cum_h)
    key_state = jnp.einsum("htd,hde->hte", key_h, carry_state, preferred_element_type=jnp.float32)
    right_side = beta_h[:, :, None] * value_h - (beta_h * start_decay)[:, :, None] * key_state
    identity_mat = jnp.eye(size_c, dtype=jnp.float32)
    new_values = jax.scipy.linalg.solve_triangular(
        identity_mat + coupling, right_side, lower=True, unit_diagonal=True
    )
    query_key = jnp.einsum("htd,hjd->htj", query_h, key_h, preferred_element_type=jnp.float32)
    query_state = jnp.einsum(
        "htd,hde->hte", query_h, carry_state, preferred_element_type=jnp.float32
    )
    output = start_decay[:, :, None] * query_state + jnp.einsum(
        "htj,hje->hte", query_key * within, new_values, preferred_element_type=jnp.float32
    )
    end_decay = cum_h[:, -1]
    tail_decay = jnp.exp(end_decay[:, None] - cum_h)
    carry_state = jnp.exp(end_decay)[:, None, None] * carry_state + jnp.einsum(
        "hjd,hje->hde",
        key_h * tail_decay[:, :, None],
        new_values,
        preferred_element_type=jnp.float32,
    )
    return (carry_state, jnp.transpose(output, (1, 0, 2)))


def delta_rule(query_rows, key_rows, value_rows, beta_rows, decay_rows):
    row_count, heads_n, key_size = query_rows.shape
    value_size = value_rows.shape[2]
    blocks = row_count // BLOCK

    def to_blocks(array_in):
        return array_in.reshape((blocks, BLOCK) + array_in.shape[1:])

    carry_state = jnp.zeros((heads_n, key_size, value_size), jnp.float32)
    unused, outputs = lax.scan(
        jax.checkpoint(block_step),
        carry_state,
        (
            to_blocks(query_rows),
            to_blocks(key_rows),
            to_blocks(value_rows),
            to_blocks(beta_rows),
            to_blocks(decay_rows),
        ),
    )
    return outputs.reshape(row_count, heads_n, value_size)


def mixer_core(
    q_raw, k_raw, v_raw, og_raw, b_raw, a_raw, conv_q, conv_k, conv_v, a_log, dt_bias, head_gain
):
    row_count = q_raw.shape[0]
    heads_n = a_log.shape[0]
    key_size = conv_q.shape[0]
    value_size = conv_v.shape[0]
    query_rows = unit_rows(
        short_conv(q_raw, conv_q).reshape(row_count, heads_n, key_size)
    ) * key_size ** (-0.5)
    key_rows = unit_rows(short_conv(k_raw, conv_k).reshape(row_count, heads_n, key_size))
    value_rows = short_conv(v_raw, conv_v).reshape(row_count, heads_n, value_size)
    beta_rows = jax.nn.sigmoid(b_raw)
    decay_rows = -jnp.exp(a_log) * jax.nn.softplus(a_raw + dt_bias)
    delta_out = delta_rule(query_rows, key_rows, value_rows, beta_rows, decay_rows)
    normed = rms_apply(delta_out, head_gain) * jax.nn.silu(
        og_raw.reshape(row_count, heads_n, value_size)
    )
    return normed.reshape(row_count, heads_n * value_size)


def shards(
    inputs,
    cotangent,
    lengths,
    norm1_gain,
    w_query,
    w_key,
    w_value,
    w_outgate,
    w_beta,
    w_alpha,
    conv_query,
    conv_key,
    conv_value,
    a_log,
    dt_bias,
    head_gain,
    w_out,
    norm2_gain,
    w_gate,
    w_up,
    w_down,
):
    local_rows = inputs[0].astype(jnp.float32)
    row_count = local_rows.shape[0]
    tensor_pos = lax.axis_index("tensor")
    positions = tensor_pos * row_count + jnp.arange(row_count, dtype=jnp.int32)
    valid_rows = (positions < lengths[0]).astype(jnp.float32)[:, None]
    (
        full_query,
        full_key,
        full_value,
        full_outgate,
        full_beta,
        full_alpha,
        full_out,
        full_gate,
        full_up,
        full_down,
        whole_convq,
        whole_convk,
        whole_convv,
    ) = (
        lax.all_gather(w_query, "dp", axis=0, tiled=True),
        lax.all_gather(w_key, "dp", axis=0, tiled=True),
        lax.all_gather(w_value, "dp", axis=0, tiled=True),
        lax.all_gather(w_outgate, "dp", axis=0, tiled=True),
        lax.all_gather(w_beta, "dp", axis=0, tiled=True),
        lax.all_gather(w_alpha, "dp", axis=0, tiled=True),
        lax.all_gather(w_out, "dp", axis=0, tiled=True),
        lax.all_gather(w_gate, "dp", axis=0, tiled=True),
        lax.all_gather(w_up, "dp", axis=0, tiled=True),
        lax.all_gather(w_down, "dp", axis=0, tiled=True),
        lax.all_gather(conv_query, "dp", axis=0, tiled=True),
        lax.all_gather(conv_key, "dp", axis=0, tiled=True),
        lax.all_gather(conv_value, "dp", axis=0, tiled=True),
    )
    heads_local = w_beta.shape[1]
    head_start = tensor_pos * heads_local
    alog_local = lax.dynamic_slice_in_dim(a_log, head_start, heads_local)
    dtb_local = lax.dynamic_slice_in_dim(dt_bias, head_start, heads_local)
    normed_one, norm_one_back = jax.vjp(rms_apply, local_rows, norm1_gain)
    rows_one = lax.all_gather(normed_one.astype(jnp.bfloat16), "tensor", axis=0, tiled=True)
    q_raw = plain_dot(rows_one, full_query)
    k_raw = plain_dot(rows_one, full_key)
    v_raw = plain_dot(rows_one, full_value)
    og_raw = plain_dot(rows_one, full_outgate)
    b_raw = plain_dot(rows_one, full_beta)
    a_raw = plain_dot(rows_one, full_alpha)
    head_out, core_back = jax.vjp(
        mixer_core,
        q_raw,
        k_raw,
        v_raw,
        og_raw,
        b_raw,
        a_raw,
        whole_convq.astype(jnp.float32),
        whole_convk.astype(jnp.float32),
        whole_convv.astype(jnp.float32),
        alog_local,
        dtb_local,
        head_gain,
    )
    head_bf = head_out.astype(jnp.bfloat16)
    part_rows = head_bf
    mixed_rows = lax.psum_scatter(
        dot_rows(part_rows, full_out), "tensor", scatter_dimension=0, tiled=True
    )
    after_mix = local_rows + mixed_rows
    normed_two, norm_two_back = jax.vjp(rms_apply, after_mix, norm2_gain)
    rows_two = lax.all_gather(normed_two.astype(jnp.bfloat16), "tensor", axis=0, tiled=True)
    gate_pre = plain_dot(rows_two, full_gate)
    up_pre = plain_dot(rows_two, full_up)
    hidden, swiglu_back = jax.vjp(swiglu, gate_pre, up_pre)
    hidden_bf = hidden.astype(jnp.bfloat16)
    part_rows = hidden_bf
    ffn_part = lax.psum_scatter(
        dot_rows(part_rows, full_down).astype(jnp.bfloat16),
        "tensor",
        scatter_dimension=0,
        tiled=True,
    ).astype(jnp.float32)
    after_ffn = after_mix + ffn_part
    outputs = (after_ffn * valid_rows).astype(jnp.bfloat16)[None]
    (
        back_query,
        back_key,
        back_value,
        back_outgate,
        back_beta,
        back_alpha,
        back_out,
        back_gate,
        back_up,
        back_down,
    ) = (
        lax.all_gather(w_query, "dp", axis=0, tiled=True),
        lax.all_gather(w_key, "dp", axis=0, tiled=True),
        lax.all_gather(w_value, "dp", axis=0, tiled=True),
        lax.all_gather(w_outgate, "dp", axis=0, tiled=True),
        lax.all_gather(w_beta, "dp", axis=0, tiled=True),
        lax.all_gather(w_alpha, "dp", axis=0, tiled=True),
        lax.all_gather(w_out, "dp", axis=0, tiled=True),
        lax.all_gather(w_gate, "dp", axis=0, tiled=True),
        lax.all_gather(w_up, "dp", axis=0, tiled=True),
        lax.all_gather(w_down, "dp", axis=0, tiled=True),
    )
    grad_after = valid_rows * cotangent[0].astype(jnp.float32)
    grad_ffn = grad_after.astype(jnp.bfloat16)
    incoming = lax.all_gather(grad_ffn, "tensor", axis=0, tiled=True)
    grad_hidden = plain_dot(incoming, back_down)
    grad_down_w = dot_tokens(incoming, hidden_bf)
    grad_hidden, grad_down_w = (grad_hidden, grad_down_w)
    grad_gate_pre, grad_up_pre = swiglu_back(grad_hidden)
    gate_low = grad_gate_pre.astype(jnp.bfloat16)
    up_low = grad_up_pre.astype(jnp.bfloat16)
    grad_gate_w = dot_tokens(rows_two, gate_low)
    grad_up_w = dot_tokens(rows_two, up_low)
    grad_normed_two = lax.psum_scatter(
        dot_rows(gate_low, back_gate) + dot_rows(up_low, back_up),
        "tensor",
        scatter_dimension=0,
        tiled=True,
    )
    grad_mid, grad_norm2 = norm_two_back(grad_normed_two)
    grad_mid = grad_mid + grad_after
    grad_mix = grad_mid.astype(jnp.bfloat16)
    incoming = lax.all_gather(grad_mix, "tensor", axis=0, tiled=True)
    grad_head = plain_dot(incoming, back_out)
    grad_out_w = dot_tokens(incoming, head_bf)
    grad_head, grad_out_w = (grad_head, grad_out_w)
    (
        grad_q_f,
        grad_k_f,
        grad_v_f,
        grad_og_f,
        grad_b_f,
        grad_a_f,
        grad_cq,
        grad_ck,
        grad_cv,
        grad_alog_local,
        grad_dtb_local,
        grad_head_gain,
    ) = core_back(grad_head)
    grad_q_low = grad_q_f.astype(jnp.bfloat16)
    grad_k_low = grad_k_f.astype(jnp.bfloat16)
    grad_v_low = grad_v_f.astype(jnp.bfloat16)
    grad_og_low = grad_og_f.astype(jnp.bfloat16)
    grad_b_low = grad_b_f.astype(jnp.bfloat16)
    grad_a_low = grad_a_f.astype(jnp.bfloat16)
    grad_query_w = dot_tokens(rows_one, grad_q_low)
    grad_key_w = dot_tokens(rows_one, grad_k_low)
    grad_value_w = dot_tokens(rows_one, grad_v_low)
    grad_outgate_w = dot_tokens(rows_one, grad_og_low)
    grad_beta_w = dot_tokens(rows_one, grad_b_low)
    grad_alpha_w = dot_tokens(rows_one, grad_a_low)
    summed = dot_rows(grad_q_low, back_query) + dot_rows(grad_k_low, back_key)
    summed = summed + dot_rows(grad_v_low, back_value) + dot_rows(grad_og_low, back_outgate)
    grad_normed_one = lax.psum_scatter(
        (summed + dot_rows(grad_b_low, back_beta) + dot_rows(grad_a_low, back_alpha)).astype(
            jnp.bfloat16
        ),
        "tensor",
        scatter_dimension=0,
        tiled=True,
    ).astype(jnp.float32)
    grad_first, grad_norm1 = norm_one_back(grad_normed_one)
    grad_inputs = (grad_mid + grad_first)[None]
    all_shards = (
        lax.psum_scatter(
            grad_query_w.astype(jnp.bfloat16), "dp", scatter_dimension=0, tiled=True
        ).astype(jnp.float32),
        lax.psum_scatter(
            grad_key_w.astype(jnp.bfloat16), "dp", scatter_dimension=0, tiled=True
        ).astype(jnp.float32),
        lax.psum_scatter(
            grad_value_w.astype(jnp.bfloat16), "dp", scatter_dimension=0, tiled=True
        ).astype(jnp.float32),
        lax.psum_scatter(
            grad_outgate_w.astype(jnp.bfloat16), "dp", scatter_dimension=0, tiled=True
        ).astype(jnp.float32),
        lax.psum_scatter(
            grad_beta_w.astype(jnp.bfloat16), "dp", scatter_dimension=0, tiled=True
        ).astype(jnp.float32),
        lax.psum_scatter(
            grad_alpha_w.astype(jnp.bfloat16), "dp", scatter_dimension=0, tiled=True
        ).astype(jnp.float32),
        lax.psum_scatter(
            grad_out_w.astype(jnp.bfloat16), "dp", scatter_dimension=0, tiled=True
        ).astype(jnp.float32),
        lax.psum_scatter(
            grad_cq.astype(jnp.bfloat16), "dp", scatter_dimension=0, tiled=True
        ).astype(jnp.float32),
        lax.psum_scatter(
            grad_ck.astype(jnp.bfloat16), "dp", scatter_dimension=0, tiled=True
        ).astype(jnp.float32),
        lax.psum_scatter(
            grad_cv.astype(jnp.bfloat16), "dp", scatter_dimension=0, tiled=True
        ).astype(jnp.float32),
        lax.psum_scatter(
            grad_gate_w.astype(jnp.bfloat16), "dp", scatter_dimension=0, tiled=True
        ).astype(jnp.float32),
        lax.psum_scatter(
            grad_up_w.astype(jnp.bfloat16), "dp", scatter_dimension=0, tiled=True
        ).astype(jnp.float32),
        lax.psum_scatter(
            grad_down_w.astype(jnp.bfloat16), "dp", scatter_dimension=0, tiled=True
        ).astype(jnp.float32),
    )
    alog_full = lax.dynamic_update_slice_in_dim(
        jnp.zeros_like(a_log), grad_alog_local, head_start, 0
    )
    dtb_full = lax.dynamic_update_slice_in_dim(
        jnp.zeros_like(dt_bias), grad_dtb_local, head_start, 0
    )
    small_sums = lax.psum(
        (grad_norm1, grad_norm2, grad_head_gain, alog_full, dtb_full), ("dp", "tensor")
    )
    return (
        outputs,
        grad_inputs,
        small_sums[0],
        all_shards[0],
        all_shards[1],
        all_shards[2],
        all_shards[3],
        all_shards[4],
        all_shards[5],
        all_shards[7],
        all_shards[8],
        all_shards[9],
        small_sums[3],
        small_sums[4],
        small_sums[2],
        all_shards[6],
        small_sums[1],
        all_shards[10],
        all_shards[11],
        all_shards[12],
    )


def solution(mesh):
    in_specs = (
        P("dp", "tensor", None),
        P("dp", "tensor", None),
        P("dp"),
        P(),
        P("dp", "tensor"),
        P("dp", "tensor"),
        P("dp", "tensor"),
        P("dp", "tensor"),
        P("dp", "tensor"),
        P("dp", "tensor"),
        P("dp", "tensor", None),
        P("dp", "tensor", None),
        P("dp", "tensor", None),
        P(),
        P(),
        P(),
        P("dp", "tensor"),
        P(),
        P("dp", "tensor"),
        P("dp", "tensor"),
        P("dp", "tensor"),
    )
    out_specs = (
        P("dp", "tensor", None),
        P("dp", "tensor", None),
        P(),
        P("dp", "tensor"),
        P("dp", "tensor"),
        P("dp", "tensor"),
        P("dp", "tensor"),
        P("dp", "tensor"),
        P("dp", "tensor"),
        P("dp", "tensor", None),
        P("dp", "tensor", None),
        P("dp", "tensor", None),
        P(),
        P(),
        P(),
        P("dp", "tensor"),
        P(),
        P("dp", "tensor"),
        P("dp", "tensor"),
        P("dp", "tensor"),
    )
    return jax.shard_map(shards, mesh=mesh, in_specs=in_specs, out_specs=out_specs, check_vma=False)
```

profile of v0, /device:TPU:0, one launch (start us, length us, event | category | flops | bytes accessed | tf_op | source)
XLA Modules:
  0.0 2830.2 jit_solution(6911755327145607036)
XLA Ops:
  16.0 32.8 %all_gather.64 = bf16[128,4,4]{2,1,0:T(4,128)(2,1)S(1)} all-gather(bf16[16,4,4]{2,1,0:T(4,128)(2,1)S(1)} %copy.363), channel_id=1, replica_groups=mesh['dp'=8,'tensor'=4] {'dp'}, dimensions={0}, use_global_device_ids=true | all-gather | bytes 4608 | tf_op jit(solution)/shard_map/all_gather | solution.py:188
  49.2 30.7 %all_gather.69 = bf16[128,4,4]{2,1,0:T(4,128)(2,1)S(1)} all-gather(bf16[16,4,4]{2,1,0:T(4,128)(2,1)S(1)} %copy.370), channel_id=1, replica_groups=mesh['dp'=8,'tensor'=4] {'dp'}, dimensions={0}, use_global_device_ids=true | all-gather | bytes 4608 | tf_op jit(solution)/shard_map/all_gather | solution.py:187
  80.2 26.0 all_gather.62
  106.4 31.3 %all_gather.67 = bf16[256,4,4]{2,1,0:T(4,128)(2,1)S(1)} all-gather(bf16[32,4,4]{2,1,0:T(4,128)(2,1)S(1)} %copy.368), channel_id=1, replica_groups=mesh['dp'=8,'tensor'=4] {'dp'}, dimensions={0}, use_global_device_ids=true | all-gather | bytes 9216 | tf_op jit(solution)/shard_map/all_gather | solution.py:189
  138.0 26.2 all_gather.65
  248.2 475.4 %while.44 = (s32[]{:T(128)}, f32[4,128,256]{2,1,0:T(8,128)S(1)}, f32[16,64,4,256]{3,1,2,0:T(8,128)}, f32[16,4,128,256]{3,2,1,0:T(8,128)}, f32[16,64,4]{2,1,0:T(8...) while((s32[]{:T(128)}, f32[4,128,256]{2,1,0:T(8,128)S(1)}, ...), condition=%wide.region_5.7_spmd.clone.clone, body=%wide.region_3.6_spmd.clone.clone.sunk | while | flops 118853952 | bytes 5871870 | solution.py:99
  251.3 19.7 custom-call.27
  281.1 19.7 custom-call.27
  310.8 19.7 custom-call.27
  340.6 19.7 custom-call.27
  400.0 19.7 custom-call.27
  429.7 19.7 custom-call.27
  459.4 19.7 custom-call.27
  518.8 19.7 custom-call.27
  548.5 19.7 custom-call.27
  607.9 19.7 custom-call.27
  637.7 19.7 custom-call.27
  697.1 19.7 custom-call.27
  763.6 69.3 %reduce-scatter.28.cloned.1.call-done = f32[256,2048]{1,0:T(8,128)} async-done(((f32[1024,2048]{1,0:T(8,128)}), f32[256,2048]{1,0:T(8,128)}) %reduce-scatter.28.cloned.1.call-update) | async-done | bytes 2097168 | tf_op jit(solution)/shard_map/reduce_scatter | solution.py:220
  839.3 88.7 %all-gather.27.cloned.1.call-done = bf16[2048,1408]{1,0:T(8,128)(2,1)} async-done(((bf16[256,1408]{1,0:T(8,128)(2,1)}), bf16[2048,1408]{1,0:T(8,128)(2,1)}) %all-gather.27.cloned.1.call-update) | async-done | bytes 5767184 | tf_op jit(solution)/shard_map/all_gather | solution.py:184
  928.0 34.9 %all-gather.25.cloned.1.call-done = bf16[1024,2048]{1,0:T(8,128)(2,1)} async-done(((bf16[256,2048]{1,0:T(8,128)(2,1)}), bf16[1024,2048]{1,0:T(8,128)(2,1)}) %all-gather.25.cloned.1.call-update) | async-done | bytes 4194320 | tf_op jit(solution)/shard_map/all_gather | solution.py:225
  974.7 83.1 %all-gather.29.cloned.1.call-done = bf16[2048,1408]{1,0:T(8,128)(2,1)} async-done(((bf16[256,1408]{1,0:T(8,128)(2,1)}), bf16[2048,1408]{1,0:T(8,128)(2,1)}) %all-gather.29.cloned.1.call-update) | async-done | bytes 5767184 | tf_op jit(solution)/shard_map/all_gather | solution.py:185
  1069.5 23.2 all-gather.33.cloned.1.call-done
  1092.7 95.0 %all-gather.31.cloned.1.call-done = bf16[2048,1408]{1,0:T(8,128)(2,1)} async-done(((bf16[256,1408]{1,0:T(8,128)(2,1)}), bf16[2048,1408]{1,0:T(8,128)(2,1)}) %all-gather.31.cloned.1.call-update) | async-done | bytes 5767184 | tf_op jit(solution)/shard_map/all_gather | solution.py:186
  1234.4 58.7 %reduce-scatter.32.cloned.1.call-done = f32[256,2048]{1,0:T(8,128)} async-done(((f32[1024,2048]{1,0:T(8,128)}), f32[256,2048]{1,0:T(8,128)}) %reduce-scatter.32.cloned.1.call-update) | async-done | bytes 2097168 | tf_op jit(solution)/shard_map/reduce_scatter | solution.py:273
  1295.9 44.2 %reduce-scatter.30.cloned.1.call-done = bf16[256,2048]{1,0:T(8,128)(2,1)} async-done(((bf16[1024,2048]{1,0:T(8,128)(2,1)}), bf16[256,2048]{1,0:T(8,128)(2,1)}) %reduce-scatter.30.cloned.1.call-update) | async-done | bytes 1048592 | tf_op jit(solution)/shard_map/reduce_scatter | solution.py:231
  1427.2 588.8 %while.43 = (s32[]{:T(128)}, f32[4,128,256]{2,1,0:T(8,128)S(1)}, f32[16,64,4,128]{3,1,2,0:T(8,128)}, f32[16,64,4,128]{3,1,2,0:T(8,128)}, f32[16,64,4,256]{3,2,1,...) while((s32[]{:T(128)}, f32[4,128,256]{2,1,0:T(8,128)S(1)}, ...), condition=%wide.region_25.27_spmd.clone, body=%wide.region_13.26_spmd.clone.sunk | while | flops 342849856 | bytes 21298192 | solution.py:99
  1433.3 19.7 custom-call.26
  1470.1 19.7 custom-call.26
  1506.9 19.7 custom-call.26
  1543.7 19.7 custom-call.26
  1580.5 19.7 custom-call.26
  1617.2 19.7 custom-call.26
  1654.1 19.7 custom-call.26
  1690.8 19.7 custom-call.26
  1727.6 19.7 custom-call.26
  1764.4 19.7 custom-call.26
  1801.2 19.7 custom-call.26
  2182.9 42.1 %reduce-scatter.60.cloned.1.call-done = bf16[32,16]{1,0:T(8,128)(2,1)} async-done(((bf16[256,16]{1,0:T(8,128)(2,1)}), bf16[32,16]{1,0:T(8,128)(2,1)}) %reduce-scatter.60.cloned.1.call-update) | async-done | bytes 1040
  2226.4 63.9 %reduce-scatter.54.cloned.1.call-done = bf16[256,4]{1,0:T(8,128)(2,1)} async-done(((bf16[2048,4]{1,0:T(8,128)(2,1)}), bf16[256,4]{1,0:T(8,128)(2,1)}) %reduce-scatter.54.cloned.1.call-update) | async-done | bytes 2064
  2291.8 63.3 %reduce-scatter.52.cloned.1.call-done = bf16[256,4]{1,0:T(8,128)(2,1)} async-done(((bf16[2048,4]{1,0:T(8,128)(2,1)}), bf16[256,4]{1,0:T(8,128)(2,1)}) %reduce-scatter.52.cloned.1.call-update) | async-done | bytes 2064
  2356.6 69.0 %reduce-scatter.38.cloned.1.call-done = bf16[256,512]{1,0:T(8,128)(2,1)} async-done(((bf16[2048,512]{1,0:T(8,128)(2,1)}), bf16[256,512]{1,0:T(8,128)(2,1)}) %reduce-scatter.38.cloned.1.call-update) | async-done | bytes 262160 | tf_op jit(solution)/shard_map/reduce_scatter | solution.py:328
  2427.5 68.9 %reduce-scatter.36.cloned.1.call-done = bf16[256,512]{1,0:T(8,128)(2,1)} async-done(((bf16[2048,512]{1,0:T(8,128)(2,1)}), bf16[256,512]{1,0:T(8,128)(2,1)}) %reduce-scatter.36.cloned.1.call-update) | async-done | bytes 262160 | tf_op jit(solution)/shard_map/reduce_scatter | solution.py:325
  2498.2 89.0 %reduce-scatter.44.cloned.1.call-done = bf16[256,1024]{1,0:T(8,128)(2,1)} async-done(((bf16[2048,1024]{1,0:T(8,128)(2,1)}), bf16[256,1024]{1,0:T(8,128)(2,1)}) %reduce-scatter.44.cloned.1.call-update) | async-done | bytes 524304 | tf_op jit(solution)/shard_map/reduce_scatter | solution.py:343
  2589.3 89.0 %reduce-scatter.40.cloned.1.call-done = bf16[256,1024]{1,0:T(8,128)(2,1)} async-done(((bf16[2048,1024]{1,0:T(8,128)(2,1)}), bf16[256,1024]{1,0:T(8,128)(2,1)}) %reduce-scatter.40.cloned.1.call-update) | async-done | bytes 524304 | tf_op jit(solution)/shard_map/reduce_scatter | solution.py:331
  2680.5 44.9 %reduce-scatter.34.cloned.1.call-done = bf16[256,2048]{1,0:T(8,128)(2,1)} async-done(((bf16[1024,2048]{1,0:T(8,128)(2,1)}), bf16[256,2048]{1,0:T(8,128)(2,1)}) %reduce-scatter.34.cloned.1.call-update) | async-done | bytes 1048592 | tf_op jit(solution)/shard_map/reduce_scatter | solution.py:314
  2727.6 42.2 %all-reduce.28 = (f32[2048]{0:T(1024)}, f32[16]{0:T(128)}, f32[16]{0:T(128)}, f32[256]{0:T(256)}, f32[2048]{0:T(1024)}) all-reduce(f32[2048]{0:T(1024)S(1)} %get-tuple-element.756, f32[16]{0:T(128)S(1)} %multiply_dynamic-update-slice_fusion, f32[16]{0:T(128)S(1)} %dynamic_update_slice.68, ...), channel_id=1, replica_groups=mesh['dp'=8,'tensor'=4] {'dp','tensor'}, use_global_device_ids=true, to_apply=%region_31.33 | all-reduce | flops 4384 | bytes 35072 | tf_op jit(solution)/shard_map/psum | solution.py:371
  2769.9 48.3 %reduce-scatter.42.cloned.1.call-done = bf16[256,1024]{1,0:T(8,128)(2,1)} async-done(((bf16[2048,1024]{1,0:T(8,128)(2,1)}), bf16[256,1024]{1,0:T(8,128)(2,1)}) %reduce-scatter.42.cloned.1.call-update) | async-done | bytes 524304 | tf_op jit(solution)/shard_map/reduce_scatter | solution.py:334
  (1638 shorter events, 1092.7 us)
Async XLA Ops:
  7.2 157.1 %all-gather.15.cloned.1.call-start = ((), (), s32[]{:S(2)}) async-start(), calls=%async_computation.18 | async-start | bytes 2359296 | tf_op jit(solution)/shard_map/all_gather | solution.py:178
  7.9 156.3 %all-gather.13.cloned.1.call-start = ((), (), s32[]{:S(2)}) async-start(), calls=%async_computation.17 | async-start | bytes 5242880 | tf_op jit(solution)/shard_map/all_gather | solution.py:196
  10.7 95.5 %copy-start.93 = (bf16[32,4,4]{0,2,1:T(4,128)(2,1)S(1)}, bf16[32,4,4]{0,2,1:T(4,128)(2,1)}, u32[]{:S(2)}) copy-start(bf16[32,4,4]{0,2,1:T(4,128)(2,1)} %param.39) | copy-start | bytes 3076
  13.3 124.7 %copy-start.95 = (bf16[256,4]{0,1:T(4,128)(2,1)S(1)}, bf16[256,4]{0,1:T(4,128)(2,1)}, u32[]{:S(2)}) copy-start(bf16[256,4]{0,1:T(4,128)(2,1)} %param.35) | copy-start | bytes 6148
  13.3 150.9 %copy-start.84 = (f32[256]{0:T(256)S(1)}, f32[256]{0:T(256)}, u32[]{:S(2)}) copy-start(f32[256]{0:T(256)} %param.42) | copy-start | bytes 3076
  13.3 164.3 %all-gather.19.cloned.1.call-start = ((), (), s32[]{:S(2)}) async-start(), calls=%async_computation.20 | async-start | bytes 2359296 | tf_op jit(solution)/shard_map/all_gather | solution.py:177
  14.0 211.3 %all-gather.17.cloned.1.call-start = ((), (), s32[]{:S(2)}) async-start(), calls=%async_computation.19 | async-start | bytes 4718592 | tf_op jit(solution)/shard_map/all_gather | solution.py:179
  14.6 725.6 %all-gather.21.cloned.1.call-start = ((), (), s32[]{:S(2)}) async-start(), calls=%async_computation.21 | async-start | bytes 4718592 | tf_op jit(solution)/shard_map/all_gather | solution.py:180
  15.2 737.8 %all-gather.23.cloned.1.call-start = ((), (), s32[]{:S(2)}) async-start(), calls=%async_computation.22 | async-start | bytes 4718592 | tf_op jit(solution)/shard_map/all_gather | solution.py:183
  15.8 817.1 %reduce-scatter.28.cloned.1.call-start = ((), (), s32[]{:S(2)}) async-start(), calls=%async_computation.23 | async-start | bytes 10485760 | tf_op jit(solution)/shard_map/reduce_scatter | solution.py:220
  49.0 120.5 %copy-start.74 = (f32[512,1]{0,1:T(1,128)}, f32[512,1]{0,1:T(1,128)S(1)}, u32[]{:S(2)}) copy-start(f32[512,1]{0,1:T(1,128)S(1)} %get-tuple-element.877) | copy-start | bytes 6148
  49.0 120.5 %copy-start.76 = (f32[512,1]{0,1:T(1,128)}, f32[512,1]{0,1:T(1,128)S(1)}, u32[]{:S(2)}) copy-start(f32[512,1]{0,1:T(1,128)S(1)} %get-tuple-element.878) | copy-start | bytes 6148
  49.0 120.5 %copy-start.78 = (f32[512,1]{0,1:T(1,128)}, f32[512,1]{0,1:T(1,128)S(1)}, u32[]{:S(2)}) copy-start(f32[512,1]{0,1:T(1,128)S(1)} %get-tuple-element.879) | copy-start | bytes 6148
  49.0 120.5 %copy-start.80 = (f32[512,1]{0,1:T(1,128)}, f32[512,1]{0,1:T(1,128)S(1)}, u32[]{:S(2)}) copy-start(f32[512,1]{0,1:T(1,128)S(1)} %get-tuple-element.880) | copy-start | bytes 6148
  80.0 102.8 %copy-start.66 = (f32[512,1]{0,1:T(1,128)}, f32[512,1]{0,1:T(1,128)S(1)}, u32[]{:S(2)}) copy-start(f32[512,1]{0,1:T(1,128)S(1)} %get-tuple-element.873) | copy-start | bytes 6148
  80.0 102.8 %copy-start.68 = (f32[512,1]{0,1:T(1,128)}, f32[512,1]{0,1:T(1,128)S(1)}, u32[]{:S(2)}) copy-start(f32[512,1]{0,1:T(1,128)S(1)} %get-tuple-element.874) | copy-start | bytes 6148
  80.0 102.8 %copy-start.70 = (f32[512,1]{0,1:T(1,128)}, f32[512,1]{0,1:T(1,128)S(1)}, u32[]{:S(2)}) copy-start(f32[512,1]{0,1:T(1,128)S(1)} %get-tuple-element.875) | copy-start | bytes 6148
  80.0 102.8 %copy-start.72 = (f32[512,1]{0,1:T(1,128)}, f32[512,1]{0,1:T(1,128)S(1)}, u32[]{:S(2)}) copy-start(f32[512,1]{0,1:T(1,128)S(1)} %get-tuple-element.876) | copy-start | bytes 6148
  80.1 119.4 %copy-start.88 = (f32[4]{0:T(128)}, f32[4]{0:T(128)S(1)}, u32[]{:S(2)}) copy-start(f32[4]{0:T(128)S(1)} %fusion.192) | copy-start | bytes 52
  762.8 165.2 %all-gather.27.cloned.1.call-start = ((), (), s32[]{:S(2)}) async-start(), calls=%async_computation.25 | async-start | bytes 6488064 | tf_op jit(solution)/shard_map/all_gather | solution.py:184
  763.5 199.3 %all-gather.25.cloned.1.call-start = ((), (), s32[]{:S(2)}) async-start(), calls=%async_computation.24 | async-start | bytes 5242880 | tf_op jit(solution)/shard_map/all_gather | solution.py:225
  836.1 221.7 %all-gather.29.cloned.1.call-start = ((), (), s32[]{:S(2)}) async-start(), calls=%async_computation.26 | async-start | bytes 6488064 | tf_op jit(solution)/shard_map/all_gather | solution.py:185
  836.7 256.1 %all-gather.33.cloned.1.call-start = ((), (), s32[]{:S(2)}) async-start(), calls=%async_computation.29 | async-start | bytes 5242880 | tf_op jit(solution)/shard_map/all_gather | solution.py:264
  838.6 349.1 %all-gather.31.cloned.1.call-start = ((), (), s32[]{:S(2)}) async-start(), calls=%async_computation.27 | async-start | bytes 6488064 | tf_op jit(solution)/shard_map/all_gather | solution.py:186
  839.2 454.0 %reduce-scatter.32.cloned.1.call-start = ((), (), s32[]{:S(2)}) async-start(), calls=%async_computation.30 | async-start | bytes 10485760 | tf_op jit(solution)/shard_map/reduce_scatter | solution.py:273
  1223.1 117.0 %reduce-scatter.30.cloned.1.call-start = ((), (), s32[]{:S(2)}) async-start(), calls=%async_computation.28 | async-start | bytes 5242880 | tf_op jit(solution)/shard_map/reduce_scatter | solution.py:231
  1234.4 153.2 %all-gather.35.cloned.1.call-start = ((), (), s32[]{:S(2)}) async-start(), calls=%async_computation.31 | async-start | bytes 5242880 | tf_op jit(solution)/shard_map/all_gather | solution.py:282
  1344.9 827.9 %reduce-scatter.46.cloned.1.call-start = ((), (), s32[]{:S(2)}) async-start(), calls=%async_computation.38 | async-start | bytes 6488064 | tf_op jit(solution)/shard_map/reduce_scatter | solution.py:355
  1356.0 819.2 %reduce-scatter.48.cloned.1.call-start = ((), (), s32[]{:S(2)}) async-start(), calls=%async_computation.39 | async-start | bytes 6488064 | tf_op jit(solution)/shard_map/reduce_scatter | solution.py:358
  1368.7 808.7 %reduce-scatter.50.cloned.1.call-start = ((), (), s32[]{:S(2)}) async-start(), calls=%async_computation.40 | async-start | bytes 6488064 | tf_op jit(solution)/shard_map/reduce_scatter | solution.py:361
  1387.5 792.6 %reduce-scatter.58.cloned.1.call-start = ((), (), s32[]{:S(2)}) async-start(), calls=%async_computation.44 | async-start | bytes 36864
  2050.7 130.8 %reduce-scatter.56.cloned.1.call-start = ((), (), s32[]{:S(2)}) async-start(), calls=%async_computation.43 | async-start | bytes 36864
  2058.8 166.2 %reduce-scatter.60.cloned.1.call-start = ((), (), s32[]{:S(2)}) async-start(), calls=%async_computation.45 | async-start | bytes 73728
  2060.1 230.2 %reduce-scatter.54.cloned.1.call-start = ((), (), s32[]{:S(2)}) async-start(), calls=%async_computation.42 | async-start | bytes 589824
  2064.3 290.8 %reduce-scatter.52.cloned.1.call-start = ((), (), s32[]{:S(2)}) async-start(), calls=%async_computation.41 | async-start | bytes 589824
  2068.4 357.3 %reduce-scatter.38.cloned.1.call-start = ((), (), s32[]{:S(2)}) async-start(), calls=%async_computation.34 | async-start | bytes 2359296 | tf_op jit(solution)/shard_map/reduce_scatter | solution.py:328
  2076.5 419.8 %reduce-scatter.36.cloned.1.call-start = ((), (), s32[]{:S(2)}) async-start(), calls=%async_computation.33 | async-start | bytes 2359296 | tf_op jit(solution)/shard_map/reduce_scatter | solution.py:325
  2085.5 501.7 %reduce-scatter.44.cloned.1.call-start = ((), (), s32[]{:S(2)}) async-start(), calls=%async_computation.37 | async-start | bytes 4718592 | tf_op jit(solution)/shard_map/reduce_scatter | solution.py:343
  2094.2 584.2 %reduce-scatter.40.cloned.1.call-start = ((), (), s32[]{:S(2)}) async-start(), calls=%async_computation.35 | async-start | bytes 4718592 | tf_op jit(solution)/shard_map/reduce_scatter | solution.py:331
  2117.5 607.8 %reduce-scatter.34.cloned.1.call-start = ((), (), s32[]{:S(2)}) async-start(), calls=%async_computation.32 | async-start | bytes 5242880 | tf_op jit(solution)/shard_map/reduce_scatter | solution.py:314
  2164.1 654.0 %reduce-scatter.42.cloned.1.call-start = ((), (), s32[]{:S(2)}) async-start(), calls=%async_computation.36 | async-start | bytes 4718592 | tf_op jit(solution)/shard_map/reduce_scatter | solution.py:334
  2179.7 545.6 %copy-start.7 = (bf16[1,256,2048]{2,1,0:T(8,128)(2,1)S(1)}, bf16[1,256,2048]{2,1,0:T(8,128)(2,1)}, u32[]{:S(2)}) copy-start(bf16[1,256,2048]{2,1,0:T(8,128)(2,1)} %param.27) | copy-start | bytes 3145732
  2179.8 545.6 %copy-start.55 = (f32[2048]{0:T(1024)S(1)}, f32[2048]{0:T(1024)}, u32[]{:S(2)}) copy-start(f32[2048]{0:T(1024)} %param.30) | copy-start | bytes 24580
  2179.8 545.6 %copy-start.83 = (f32[256]{0:T(256)S(1)}, f32[256]{0:T(256)}, u32[]{:S(2)}) copy-start(f32[256]{0:T(256)} %copy-done.82) | copy-start | bytes 3076
  2427.5 300.1 %copy-start.65 = (f32[2048]{0:T(1024)S(1)}, f32[2048]{0:T(1024)}, u32[]{:S(2)}) copy-start(f32[2048]{0:T(1024)} %get-tuple-element.746) | copy-start | bytes 24580
  2427.5 300.1 %copy-start.90 = (f32[256]{0:T(256)S(1)}, f32[256]{0:T(256)}, u32[]{:S(2)}) copy-start(f32[256]{0:T(256)} %get-tuple-element.740) | copy-start | bytes 3076
  2427.5 342.3 %copy-start.87 = (f32[256]{0:T(256)S(1)}, f32[256]{0:T(256)}, u32[]{:S(2)}) copy-start(f32[256]{0:T(256)} %copy-done.86) | copy-start | bytes 3076
  2589.3 230.9 %copy-start.20 = (f32[256,2048]{1,0:T(8,128)S(1)}, f32[256,2048]{1,0:T(8,128)}, u32[]{:S(2)}) copy-start(f32[256,2048]{1,0:T(8,128)} %get-tuple-element.828) | copy-start | bytes 6291460
  (92 other events, 1248.6 us)
Sparse Core Ops, SparseCore 0:
  10.1 53.4 all-gather.14
  65.8 33.0 all-gather.12
  101.0 49.7 all-gather.18
  152.8 72.5 all-gather.16
  227.3 72.1 all-gather.20
  301.4 72.1 all-gather.22
  762.9 69.9 reduce-scatter.27
  835.3 92.6 all-gather.26
  930.2 32.6 all-gather.24
  965.1 92.6 all-gather.28
  1060.0 32.6 all-gather.32
  1095.0 92.6 all-gather.30
  1223.2 69.9 reduce-scatter.31
  1295.6 44.4 reduce-scatter.29
  1345.0 34.4 all-gather.34
  1383.5 110.0 reduce-scatter.45
  1497.5 109.5 reduce-scatter.47
  1611.0 110.0 reduce-scatter.49
  2050.8 53.6 reduce-scatter.57
  2107.8 52.5 reduce-scatter.55
  2164.7 60.2 reduce-scatter.59
  2229.3 60.9 reduce-scatter.53
  2294.2 60.8 reduce-scatter.51
  2358.9 66.7 reduce-scatter.37
  2429.6 66.6 reduce-scatter.35
  2500.3 86.8 reduce-scatter.43
  2590.7 87.6 reduce-scatter.39
  2681.0 44.2 reduce-scatter.33
  2729.0 89.1 reduce-scatter.41
where the time goes:
time: 2840 us; the launch traced here: 2830 us
  waiting for transfers between devices  1100 us (39%)
  other arithmetic  805 us (28%)
  matrix products  475 us (17%)
  local copies, waits for them, and re-layouts  241 us (8%)
  blocking collectives  189 us (7%)
    another operation x128, other arithmetic, block_step(): jax.scipy.linalg.solve_triangular(identity_mat + coupling, right_side, lo...  634 us
    unnamed x34, waiting for transfers between devices  174 us
    squeeze x112, local copies, waits for them, and re-layouts, delta_rule(): lax.scan(jax.checkpoint(block_step), carry_state, (to_blocks(query_rows),...  98.1 us
    all_gather x1, waiting for transfers between devices, shards(): lax.all_gather(w_down, 'dp', axis=0, tiled=True)  95 us
    dot_general x10, matrix products, plain_dot(): return jnp.dot(left_mat, right_mat, preferred_element_type=jnp.float32)  90.6 us
    reduce_scatter x1, waiting for transfers between devices, shards(): lax.psum_scatter(grad_out_w.astype(jnp.bfloat16), 'dp', scatter_dimension...  89 us
    reduce_scatter x1, waiting for transfers between devices, shards(): lax.psum_scatter(grad_value_w.astype(jnp.bfloat16), 'dp', scatter_dimensi...  89 us
    all_gather x1, waiting for transfers between devices, shards(): lax.all_gather(w_gate, 'dp', axis=0, tiled=True)  88.7 us
  transfers between devices with their start and end apart: 29, of which 18 were waited for; matrix products, arithmetic and copies ran while one was open for 51% of the time, Pallas kernels for 0%

commit v1 on v0

--- a/solution.py
+++ b/solution.py
@@ -4,6 +4,21 @@
 from jax.sharding import PartitionSpec as P
 
 BLOCK = 64
+
+
+def _resolve_object(vals, bus_axis):
+    width = lax.axis_size(bus_axis)
+    pile = [vals]
+    for it in range(1, width):
+        pile.append(
+            lax.ppermute(
+                pile[it - 1],
+                axis_name=bus_axis,
+                perm=[(kk, (kk - 1) % width) for kk in range(width)],
+            )
+        )
+    piece_now = jnp.concatenate(pile, axis=0)
+    return jnp.roll(piece_now, lax.axis_index(bus_axis) * vals.shape[0], 0)
 
 
 def plain_dot(left_mat, right_mat):
@@ -181,7 +196,7 @@
         lax.all_gather(w_beta, "dp", axis=0, tiled=True),
         lax.all_gather(w_alpha, "dp", axis=0, tiled=True),
         lax.all_gather(w_out, "dp", axis=0, tiled=True),
-        lax.all_gather(w_gate, "dp", axis=0, tiled=True),
+        _resolve_object(w_gate, "dp"),
         lax.all_gather(w_up, "dp", axis=0, tiled=True),
         lax.all_gather(w_down, "dp", axis=0, tiled=True),
         lax.all_gather(conv_query, "dp", axis=0, tiled=True),

time: 2840 us -> 2900 us (1.021)
  starting transfers between devices: 1.64 us -> 37.1 us
    ppermute x0 -> x7, waiting for transfers between devices: none -> 144 us  [_resolve_object(): lax.ppermute(pile[it - 1], axis_name=bus_axis, perm=[(kk, (kk - 1) % widt...]
    all_gather x1, waiting for transfers between devices: 95 us -> 0.01 us  [shards(): lax.all_gather(w_down, 'dp', axis=0, tiled=True)]
    ppermute x0 -> x7, starting transfers between devices: none -> 35.3 us  [_resolve_object(): lax.ppermute(pile[it - 1], axis_name=bus_axis, perm=[(kk, (kk - 1) % widt...]
    unnamed x245 -> x278, local copies, waits for them, and re-layouts: 40.9 us -> 62.6 us
  transfers between devices with their start and end apart: 29 -> 36, of which waited for: 18 -> 23; matrix products, arithmetic and copies ran while one was open for 51% -> 52% of each run, Pallas kernels for 0% -> 0%
where the time goes in v1:
time: 2900 us; the launch traced here: 2880 us
  waiting for transfers between devices  1090 us (38%)
  other arithmetic  808 us (28%)
  matrix products  474 us (16%)
  local copies, waits for them, and re-layouts  263 us (9%)
  blocking collectives  189 us (7%)
  starting transfers between devices  37.1 us (1%)
    another operation x128, other arithmetic, block_step(): jax.scipy.linalg.solve_triangular(identity_mat + coupling, right_side, lo...  634 us
    unnamed x34, waiting for transfers between devices  175 us
    ppermute x7, waiting for transfers between devices, _resolve_object(): lax.ppermute(pile[it - 1], axis_name=bus_axis, perm=[(kk, (kk - 1) % widt...  144 us
    squeeze x112, local copies, waits for them, and re-layouts, delta_rule(): lax.scan(jax.checkpoint(block_step), carry_state, (to_blocks(query_rows),...  98.1 us
    dot_general x10, matrix products, plain_dot(): return jnp.dot(left_mat, right_mat, preferred_element_type=jnp.float32)  90.4 us
    reduce_scatter x1, waiting for transfers between devices, shards(): lax.psum_scatter(grad_value_w.astype(jnp.bfloat16), 'dp', scatter_dimensi...  89.1 us
    reduce_scatter x1, waiting for transfers between devices, shards(): lax.psum_scatter(grad_out_w.astype(jnp.bfloat16), 'dp', scatter_dimension...  89 us
    dot_general x10, matrix products, dot_rows(): lax.dot_general(left_mat, right_mat, (((1,), (1,)), ((), ())), preferred_...  86 us
  transfers between devices with their start and end apart: 36, of which 23 were waited for; matrix products, arithmetic and copies ran while one was open for 52% of the time, Pallas kernels for 0%

profile of v1, /device:TPU:0, one launch (start us, length us, event | category | flops | bytes accessed | tf_op | source)
XLA Modules:
  0.0 2883.6 jit_solution(14716004856339613388)
XLA Ops:
  16.0 32.7 %all_gather.63 = bf16[128,4,4]{2,1,0:T(4,128)(2,1)S(1)} all-gather(bf16[16,4,4]{2,1,0:T(4,128)(2,1)S(1)} %copy.363), channel_id=1, replica_groups=mesh['dp'=8,'tensor'=4] {'dp'}, dimensions={0}, use_global_device_ids=true | all-gather | bytes 4608 | tf_op jit(solution)/shard_map/all_gather | solution.py:203
  49.1 30.6 %all_gather.68 = bf16[128,4,4]{2,1,0:T(4,128)(2,1)S(1)} all-gather(bf16[16,4,4]{2,1,0:T(4,128)(2,1)S(1)} %copy.370), channel_id=1, replica_groups=mesh['dp'=8,'tensor'=4] {'dp'}, dimensions={0}, use_global_device_ids=true | all-gather | bytes 4608 | tf_op jit(solution)/shard_map/all_gather | solution.py:202
  80.1 26.0 all_gather.61
  106.2 31.6 %all_gather.66 = bf16[256,4,4]{2,1,0:T(4,128)(2,1)S(1)} all-gather(bf16[32,4,4]{2,1,0:T(4,128)(2,1)S(1)} %copy.368), channel_id=1, replica_groups=mesh['dp'=8,'tensor'=4] {'dp'}, dimensions={0}, use_global_device_ids=true | all-gather | bytes 9216 | tf_op jit(solution)/shard_map/all_gather | solution.py:204
  138.1 26.1 all_gather.64
  248.4 475.4 %while.44 = (s32[]{:T(128)}, f32[4,128,256]{2,1,0:T(8,128)S(1)}, f32[16,64,4,256]{3,1,2,0:T(8,128)}, f32[16,4,128,256]{3,2,1,0:T(8,128)}, f32[16,64,4]{2,1,0:T(8...) while((s32[]{:T(128)}, f32[4,128,256]{2,1,0:T(8,128)S(1)}, ...), condition=%wide.region_5.7_spmd.clone.clone, body=%wide.region_3.6_spmd.clone.clone.sunk | while | flops 118853952 | bytes 5871870 | solution.py:114
  281.3 19.7 custom-call.29
  311.0 19.7 custom-call.29
  340.8 19.7 custom-call.29
  429.9 19.7 custom-call.29
  489.4 19.7 custom-call.29
  519.1 19.7 custom-call.29
  548.8 19.7 custom-call.29
  578.5 19.7 custom-call.29
  608.2 19.7 custom-call.29
  637.9 19.7 custom-call.29
  667.6 19.7 custom-call.29
  697.3 19.7 custom-call.29
  766.6 66.3 %reduce-scatter.28.cloned.1.call-done = f32[256,2048]{1,0:T(8,128)} async-done(((f32[1024,2048]{1,0:T(8,128)}), f32[256,2048]{1,0:T(8,128)}) %reduce-scatter.28.cloned.1.call-update) | async-done | bytes 2097168 | tf_op jit(solution)/shard_map/reduce_scatter | solution.py:235
  880.9 29.4 %collective-permute-done.2 = bf16[256,1408]{1,0:T(8,128)(2,1)S(1)} collective-permute-done((bf16[256,1408]{1,0:T(8,128)(2,1)S(1)}, bf16[256,1408]{1,0:T(8,128)(2,1)S(1)}, u32[]{:S(2)}, u32[]{:S(2)}) %collective-permute-start.2) | collective-permute-done | bytes 720928 | tf_op jit(solution)/shard_map/ppermute | solution.py:14
  940.8 27.6 collective-permute-done.4
  978.7 25.4 collective-permute-done.5
  1051.7 72.9 %all-gather.27.cloned.1.call-done = bf16[2048,1408]{1,0:T(8,128)(2,1)} async-done(((bf16[256,1408]{1,0:T(8,128)(2,1)}), bf16[2048,1408]{1,0:T(8,128)(2,1)}) %all-gather.27.cloned.1.call-update) | async-done | bytes 5767184 | tf_op jit(solution)/shard_map/all_gather | solution.py:200
  1124.6 34.9 %all-gather.25.cloned.1.call-done = bf16[1024,2048]{1,0:T(8,128)(2,1)} async-done(((bf16[256,2048]{1,0:T(8,128)(2,1)}), bf16[1024,2048]{1,0:T(8,128)(2,1)}) %all-gather.25.cloned.1.call-update) | async-done | bytes 4194320 | tf_op jit(solution)/shard_map/all_gather | solution.py:240
  1186.2 68.3 %all-gather.33.cloned.1.call-done = bf16[2048,1408]{1,0:T(8,128)(2,1)} async-done(((bf16[256,1408]{1,0:T(8,128)(2,1)}), bf16[2048,1408]{1,0:T(8,128)(2,1)}) %all-gather.33.cloned.1.call-update) | async-done | bytes 5767184 | tf_op jit(solution)/shard_map/all_gather | solution.py:273
  1284.8 58.6 %reduce-scatter.32.cloned.1.call-done = f32[256,2048]{1,0:T(8,128)} async-done(((f32[1024,2048]{1,0:T(8,128)}), f32[256,2048]{1,0:T(8,128)}) %reduce-scatter.32.cloned.1.call-update) | async-done | bytes 2097168 | tf_op jit(solution)/shard_map/reduce_scatter | solution.py:288
  1346.1 44.2 %reduce-scatter.30.cloned.1.call-done = bf16[256,2048]{1,0:T(8,128)(2,1)} async-done(((bf16[1024,2048]{1,0:T(8,128)(2,1)}), bf16[256,2048]{1,0:T(8,128)(2,1)}) %reduce-scatter.30.cloned.1.call-update) | async-done | bytes 1048592 | tf_op jit(solution)/shard_map/reduce_scatter | solution.py:246
  1477.7 589.0 %while.43 = (s32[]{:T(128)}, f32[4,128,256]{2,1,0:T(8,128)S(1)}, f32[16,64,4,128]{3,1,2,0:T(8,128)}, f32[16,64,4,128]{3,1,2,0:T(8,128)}, f32[16,64,4,256]{3,2,1,...) while((s32[]{:T(128)}, f32[4,128,256]{2,1,0:T(8,128)S(1)}, ...), condition=%wide.region_25.27_spmd.clone, body=%wide.region_13.26_spmd.clone.sunk | while | flops 342849856 | bytes 21298192 | solution.py:114
  1483.8 19.7 custom-call.28
  1520.6 19.7 custom-call.28
  1557.4 19.7 custom-call.28
  1594.2 19.7 custom-call.28
  1631.0 19.7 custom-call.28
  1704.6 19.7 custom-call.28
  1741.4 19.7 custom-call.28
  1778.1 19.7 custom-call.28
  1814.9 19.7 custom-call.28
  1851.7 19.7 custom-call.28
  2234.6 43.6 %reduce-scatter.60.cloned.1.call-done = bf16[32,16]{1,0:T(8,128)(2,1)} async-done(((bf16[256,16]{1,0:T(8,128)(2,1)}), bf16[32,16]{1,0:T(8,128)(2,1)}) %reduce-scatter.60.cloned.1.call-update) | async-done | bytes 1040
  2279.6 63.8 %reduce-scatter.54.cloned.1.call-done = bf16[256,4]{1,0:T(8,128)(2,1)} async-done(((bf16[2048,4]{1,0:T(8,128)(2,1)}), bf16[256,4]{1,0:T(8,128)(2,1)}) %reduce-scatter.54.cloned.1.call-update) | async-done | bytes 2064
  2345.0 63.4 %reduce-scatter.52.cloned.1.call-done = bf16[256,4]{1,0:T(8,128)(2,1)} async-done(((bf16[2048,4]{1,0:T(8,128)(2,1)}), bf16[256,4]{1,0:T(8,128)(2,1)}) %reduce-scatter.52.cloned.1.call-update) | async-done | bytes 2064
  2409.9 68.9 %reduce-scatter.38.cloned.1.call-done = bf16[256,512]{1,0:T(8,128)(2,1)} async-done(((bf16[2048,512]{1,0:T(8,128)(2,1)}), bf16[256,512]{1,0:T(8,128)(2,1)}) %reduce-scatter.38.cloned.1.call-update) | async-done | bytes 262160 | tf_op jit(solution)/shard_map/reduce_scatter | solution.py:343
  2480.6 68.8 %reduce-scatter.36.cloned.1.call-done = bf16[256,512]{1,0:T(8,128)(2,1)} async-done(((bf16[2048,512]{1,0:T(8,128)(2,1)}), bf16[256,512]{1,0:T(8,128)(2,1)}) %reduce-scatter.36.cloned.1.call-update) | async-done | bytes 262160 | tf_op jit(solution)/shard_map/reduce_scatter | solution.py:340
  2551.3 89.0 %reduce-scatter.44.cloned.1.call-done = bf16[256,1024]{1,0:T(8,128)(2,1)} async-done(((bf16[2048,1024]{1,0:T(8,128)(2,1)}), bf16[256,1024]{1,0:T(8,128)(2,1)}) %reduce-scatter.44.cloned.1.call-update) | async-done | bytes 524304 | tf_op jit(solution)/shard_map/reduce_scatter | solution.py:358
  2642.4 89.1 %reduce-scatter.40.cloned.1.call-done = bf16[256,1024]{1,0:T(8,128)(2,1)} async-done(((bf16[2048,1024]{1,0:T(8,128)(2,1)}), bf16[256,1024]{1,0:T(8,128)(2,1)}) %reduce-scatter.40.cloned.1.call-update) | async-done | bytes 524304 | tf_op jit(solution)/shard_map/reduce_scatter | solution.py:346
  2733.6 44.9 %reduce-scatter.34.cloned.1.call-done = bf16[256,2048]{1,0:T(8,128)(2,1)} async-done(((bf16[1024,2048]{1,0:T(8,128)(2,1)}), bf16[256,2048]{1,0:T(8,128)(2,1)}) %reduce-scatter.34.cloned.1.call-update) | async-done | bytes 1048592 | tf_op jit(solution)/shard_map/reduce_scatter | solution.py:329
  2780.7 42.2 %all-reduce.28 = (f32[2048]{0:T(1024)}, f32[16]{0:T(128)}, f32[16]{0:T(128)}, f32[256]{0:T(256)}, f32[2048]{0:T(1024)}) all-reduce(f32[2048]{0:T(1024)S(1)} %get-tuple-element.756, f32[16]{0:T(128)S(1)} %multiply_dynamic-update-slice_fusion, f32[16]{0:T(128)S(1)} %dynamic_update_slice.68, ...), channel_id=1, replica_groups=mesh['dp'=8,'tensor'=4] {'dp','tensor'}, use_global_device_ids=true, to_apply=%region_31.33 | all-reduce | flops 4384 | bytes 35072 | tf_op jit(solution)/shard_map/psum | solution.py:386
  2822.9 48.4 %reduce-scatter.42.cloned.1.call-done = bf16[256,1024]{1,0:T(8,128)(2,1)} async-done(((bf16[2048,1024]{1,0:T(8,128)(2,1)}), bf16[256,1024]{1,0:T(8,128)(2,1)}) %reduce-scatter.42.cloned.1.call-update) | async-done | bytes 524304 | tf_op jit(solution)/shard_map/reduce_scatter | solution.py:349
  (1686 shorter events, 1233.1 us)
Async XLA Ops:
  7.3 157.1 %all-gather.15.cloned.1.call-start = ((), (), s32[]{:S(2)}) async-start(), calls=%async_computation.18 | async-start | bytes 2359296 | tf_op jit(solution)/shard_map/all_gather | solution.py:193
  8.0 156.4 %all-gather.13.cloned.1.call-start = ((), (), s32[]{:S(2)}) async-start(), calls=%async_computation.17 | async-start | bytes 5242880 | tf_op jit(solution)/shard_map/all_gather | solution.py:211
  10.7 127.4 %copy-start.103 = (bf16[256,4]{0,1:T(4,128)(2,1)S(1)}, bf16[256,4]{0,1:T(4,128)(2,1)}, u32[]{:S(2)}) copy-start(bf16[256,4]{0,1:T(4,128)(2,1)} %param.35) | copy-start | bytes 6148
  10.7 153.5 %copy-start.88 = (f32[256]{0:T(256)S(1)}, f32[256]{0:T(256)}, u32[]{:S(2)}) copy-start(f32[256]{0:T(256)} %param.42) | copy-start | bytes 3076
  13.3 164.5 %all-gather.19.cloned.1.call-start = ((), (), s32[]{:S(2)}) async-start(), calls=%async_computation.20 | async-start | bytes 2359296 | tf_op jit(solution)/shard_map/all_gather | solution.py:192
  14.0 211.2 %all-gather.17.cloned.1.call-start = ((), (), s32[]{:S(2)}) async-start(), calls=%async_computation.19 | async-start | bytes 4718592 | tf_op jit(solution)/shard_map/all_gather | solution.py:194
  14.6 725.5 %all-gather.21.cloned.1.call-start = ((), (), s32[]{:S(2)}) async-start(), calls=%async_computation.21 | async-start | bytes 4718592 | tf_op jit(solution)/shard_map/all_gather | solution.py:195
  15.2 737.8 %all-gather.23.cloned.1.call-start = ((), (), s32[]{:S(2)}) async-start(), calls=%async_computation.22 | async-start | bytes 4718592 | tf_op jit(solution)/shard_map/all_gather | solution.py:198
  15.8 817.1 %reduce-scatter.28.cloned.1.call-start = ((), (), s32[]{:S(2)}) async-start(), calls=%async_computation.23 | async-start | bytes 10485760 | tf_op jit(solution)/shard_map/reduce_scatter | solution.py:235
  48.9 120.7 %copy-start.78 = (f32[512,1]{0,1:T(1,128)}, f32[512,1]{0,1:T(1,128)S(1)}, u32[]{:S(2)}) copy-start(f32[512,1]{0,1:T(1,128)S(1)} %get-tuple-element.877) | copy-start | bytes 6148
  48.9 120.7 %copy-start.80 = (f32[512,1]{0,1:T(1,128)}, f32[512,1]{0,1:T(1,128)S(1)}, u32[]{:S(2)}) copy-start(f32[512,1]{0,1:T(1,128)S(1)} %get-tuple-element.878) | copy-start | bytes 6148
  164.3 575.8 %copy-start.100 = (f32[1,2,4,128]{3,1,2,0:T(2,128)}, f32[1,2,4,128]{3,1,2,0:T(2,128)S(1)}, u32[]{:S(2)}) copy-start(f32[1,2,4,128]{3,1,2,0:T(2,128)S(1)} %copy.491) | copy-start | bytes 12292
  762.8 276.8 %all-gather.31.cloned.1.call-start = ((), (), s32[]{:S(2)}) async-start(), calls=%async_computation.28 | async-start | bytes 5242880 | tf_op jit(solution)/shard_map/all_gather | solution.py:279
  765.2 274.4 %all-gather.29.cloned.1.call-start = ((), (), s32[]{:S(2)}) async-start(), calls=%async_computation.26 | async-start | bytes 6488064 | tf_op jit(solution)/shard_map/all_gather | solution.py:201
  766.0 358.7 %all-gather.27.cloned.1.call-start = ((), (), s32[]{:S(2)}) async-start(), calls=%async_computation.25 | async-start | bytes 6488064 | tf_op jit(solution)/shard_map/all_gather | solution.py:200
  766.5 393.0 %all-gather.25.cloned.1.call-start = ((), (), s32[]{:S(2)}) async-start(), calls=%async_computation.24 | async-start | bytes 5242880 | tf_op jit(solution)/shard_map/all_gather | solution.py:240
  836.1 418.4 %all-gather.33.cloned.1.call-start = ((), (), s32[]{:S(2)}) async-start(), calls=%async_computation.29 | async-start | bytes 6488064 | tf_op jit(solution)/shard_map/all_gather | solution.py:273
  836.2 20.0 collective-permute-start
  856.2 19.6 collective-permute-start.1
  875.8 34.6 %collective-permute-start.2 = (bf16[256,1408]{1,0:T(8,128)(2,1)S(1)}, bf16[256,1408]{1,0:T(8,128)(2,1)S(1)}, u32[]{:S(2)}, u32[]{:S(2)}) collective-permute-start(bf16[256,1408]{1,0:T(8,128)(2,1)S(1)} %collective-permute-done.1), channel_id=1, source_target_pairs={{0,28},{4,0},{8,4},{12,8},{16,12},{20,16},{24,20},{28,24},{1,29},{... | collective-permute-start | bytes 2162696 | tf_op jit(solution)/shard_map/ppermute | solution.py:14
  911.2 22.0 collective-permute-start.3
  933.1 35.3 %collective-permute-start.4 = (bf16[256,1408]{1,0:T(8,128)(2,1)}, bf16[256,1408]{1,0:T(8,128)(2,1)}, u32[]{:S(2)}, u32[]{:S(2)}) collective-permute-start(bf16[256,1408]{1,0:T(8,128)(2,1)} %collective-permute-done.3), channel_id=1, source_target_pairs={{0,28},{4,0},{8,4},{12,8},{16,12},{20,16},{24,20},{28,24},{1,29},{... | collective-permute-start | bytes 2162696 | tf_op jit(solution)/shard_map/ppermute | solution.py:14
  938.5 404.9 %reduce-scatter.32.cloned.1.call-start = ((), (), s32[]{:S(2)}) async-start(), calls=%async_computation.30 | async-start | bytes 10485760 | tf_op jit(solution)/shard_map/reduce_scatter | solution.py:288
  968.4 35.6 %collective-permute-start.5 = (bf16[256,1408]{1,0:T(8,128)(2,1)}, bf16[256,1408]{1,0:T(8,128)(2,1)S(1)}, u32[]{:S(2)}, u32[]{:S(2)}) collective-permute-start(bf16[256,1408]{1,0:T(8,128)(2,1)} %collective-permute-done.4), channel_id=1, source_target_pairs={{0,28},{4,0},{8,4},{12,8},{16,12},{20,16},{24,20},{28,24},{1,29},{... | collective-permute-start | bytes 2162696 | tf_op jit(solution)/shard_map/ppermute | solution.py:14
  1004.1 25.0 collective-permute-start.6
  1273.3 117.0 %reduce-scatter.30.cloned.1.call-start = ((), (), s32[]{:S(2)}) async-start(), calls=%async_computation.27 | async-start | bytes 5242880 | tf_op jit(solution)/shard_map/reduce_scatter | solution.py:246
  1284.8 152.9 %all-gather.35.cloned.1.call-start = ((), (), s32[]{:S(2)}) async-start(), calls=%async_computation.31 | async-start | bytes 5242880 | tf_op jit(solution)/shard_map/all_gather | solution.py:297
  1395.1 829.3 %reduce-scatter.46.cloned.1.call-start = ((), (), s32[]{:S(2)}) async-start(), calls=%async_computation.38 | async-start | bytes 6488064 | tf_op jit(solution)/shard_map/reduce_scatter | solution.py:370
  1406.2 820.6 %reduce-scatter.48.cloned.1.call-start = ((), (), s32[]{:S(2)}) async-start(), calls=%async_computation.39 | async-start | bytes 6488064 | tf_op jit(solution)/shard_map/reduce_scatter | solution.py:373
  1418.9 810.3 %reduce-scatter.50.cloned.1.call-start = ((), (), s32[]{:S(2)}) async-start(), calls=%async_computation.40 | async-start | bytes 6488064 | tf_op jit(solution)/shard_map/reduce_scatter | solution.py:376
  1437.5 794.3 %reduce-scatter.58.cloned.1.call-start = ((), (), s32[]{:S(2)}) async-start(), calls=%async_computation.44 | async-start | bytes 36864
  2103.9 129.3 %reduce-scatter.56.cloned.1.call-start = ((), (), s32[]{:S(2)}) async-start(), calls=%async_computation.43 | async-start | bytes 36864
  2111.8 166.4 %reduce-scatter.60.cloned.1.call-start = ((), (), s32[]{:S(2)}) async-start(), calls=%async_computation.45 | async-start | bytes 73728
  2113.1 230.4 %reduce-scatter.54.cloned.1.call-start = ((), (), s32[]{:S(2)}) async-start(), calls=%async_computation.42 | async-start | bytes 589824
  2117.3 291.1 %reduce-scatter.52.cloned.1.call-start = ((), (), s32[]{:S(2)}) async-start(), calls=%async_computation.41 | async-start | bytes 589824
  2121.3 357.6 %reduce-scatter.38.cloned.1.call-start = ((), (), s32[]{:S(2)}) async-start(), calls=%async_computation.34 | async-start | bytes 2359296 | tf_op jit(solution)/shard_map/reduce_scatter | solution.py:343
  2129.4 420.1 %reduce-scatter.36.cloned.1.call-start = ((), (), s32[]{:S(2)}) async-start(), calls=%async_computation.33 | async-start | bytes 2359296 | tf_op jit(solution)/shard_map/reduce_scatter | solution.py:340
  2136.8 503.5 %reduce-scatter.44.cloned.1.call-start = ((), (), s32[]{:S(2)}) async-start(), calls=%async_computation.37 | async-start | bytes 4718592 | tf_op jit(solution)/shard_map/reduce_scatter | solution.py:358
  2145.5 585.9 %reduce-scatter.40.cloned.1.call-start = ((), (), s32[]{:S(2)}) async-start(), calls=%async_computation.35 | async-start | bytes 4718592 | tf_op jit(solution)/shard_map/reduce_scatter | solution.py:346
  2168.8 609.6 %reduce-scatter.34.cloned.1.call-start = ((), (), s32[]{:S(2)}) async-start(), calls=%async_computation.32 | async-start | bytes 5242880 | tf_op jit(solution)/shard_map/reduce_scatter | solution.py:329
  2215.7 655.6 %reduce-scatter.42.cloned.1.call-start = ((), (), s32[]{:S(2)}) async-start(), calls=%async_computation.36 | async-start | bytes 4718592 | tf_op jit(solution)/shard_map/reduce_scatter | solution.py:349
  2226.8 551.7 %copy-start.7 = (bf16[1,256,2048]{2,1,0:T(8,128)(2,1)S(1)}, bf16[1,256,2048]{2,1,0:T(8,128)(2,1)}, u32[]{:S(2)}) copy-start(bf16[1,256,2048]{2,1,0:T(8,128)(2,1)} %param.27) | copy-start | bytes 3145732
  2226.8 551.7 %copy-start.59 = (f32[2048]{0:T(1024)S(1)}, f32[2048]{0:T(1024)}, u32[]{:S(2)}) copy-start(f32[2048]{0:T(1024)} %param.30) | copy-start | bytes 24580
  2226.8 551.7 %copy-start.87 = (f32[256]{0:T(256)S(1)}, f32[256]{0:T(256)}, u32[]{:S(2)}) copy-start(f32[256]{0:T(256)} %copy-done.86) | copy-start | bytes 3076
  2229.2 551.5 %copy-start.69 = (f32[2048]{0:T(1024)S(1)}, f32[2048]{0:T(1024)}, u32[]{:S(2)}) copy-start(f32[2048]{0:T(1024)} %get-tuple-element.746) | copy-start | bytes 24580
  2229.2 551.5 %copy-start.96 = (f32[256]{0:T(256)S(1)}, f32[256]{0:T(256)}, u32[]{:S(2)}) copy-start(f32[256]{0:T(256)} %get-tuple-element.740) | copy-start | bytes 3076
  2229.2 593.7 %copy-start.91 = (f32[256]{0:T(256)S(1)}, f32[256]{0:T(256)}, u32[]{:S(2)}) copy-start(f32[256]{0:T(256)} %copy-done.90) | copy-start | bytes 3076
  2409.9 463.5 %copy-start.21 = (f32[256,2048]{1,0:T(8,128)S(1)}, f32[256,2048]{1,0:T(8,128)}, u32[]{:S(2)}) copy-start(f32[256,2048]{1,0:T(8,128)} %get-tuple-element.828) | copy-start | bytes 6291460
  (108 other events, 2583.1 us)
Sparse Core Ops, SparseCore 0:
  10.2 53.4 all-gather.14
  65.8 33.0 all-gather.12
  101.0 49.6 all-gather.18
  152.7 72.4 all-gather.16
  227.2 72.4 all-gather.20
  301.7 72.0 all-gather.22
  762.9 69.9 reduce-scatter.27
  835.1 34.4 all-gather.30
  872.1 151.7 all-gather.28
  1026.1 98.4 all-gather.26
  1126.9 32.6 all-gather.24
  1161.8 92.6 all-gather.32
  1273.4 69.9 reduce-scatter.31
  1345.8 44.4 reduce-scatter.29
  1395.2 34.4 all-gather.34
  1433.7 110.1 reduce-scatter.45
  1547.8 109.6 reduce-scatter.47
  1661.5 110.0 reduce-scatter.49
  2104.1 53.5 reduce-scatter.57
  2161.0 52.5 reduce-scatter.55
  2217.9 60.2 reduce-scatter.59
  2282.5 60.8 reduce-scatter.53
  2347.4 60.9 reduce-scatter.51
  2412.2 66.6 reduce-scatter.37
  2482.8 66.6 reduce-scatter.35
  2553.4 86.8 reduce-scatter.43
  2643.8 87.6 reduce-scatter.39
  2734.2 44.2 reduce-scatter.33
  2782.1 89.1 reduce-scatter.41
